TPU v7x, 32 devices: a whole 2x2x4 slice. The times are simulated.
32 devices in a mesh: row: 4 (over y, core), col: 8 (over z, x).
Axes of the slice: x: 2, y: 2, z: 4, core: 2. Of those that a mesh axis runs over, the one named last changes fastest.
Arguments:
- phases: int32 [4, 8, 8, 24, 576], P('row', 'col'), may hold values from 0 to 2
- grain: float32 [4, 8, 8, 24, 576], P('row', 'col'), may hold values from 0.5 to 2
- phase_cond: float32 [3], replicated, may hold values from 0.3 to 3
- micro_counts: int32 [4, 8, 8], P('row', 'col'), may hold values from 6 to 12, as said below
- current: float32 [4, 8, 8], P('row', 'col'), may hold values from -5 to 5
- load: float32 [4, 8, 8], P('row', 'col'), may hold values from -16 to 16
Outputs:
- states: float32 [4, 8, 8, 3, 24, 576], P('row', 'col')
- tangent: float32 [4, 8, 8, 3, 3], P('row', 'col')
- increment: float32 [4, 8, 8], P('row', 'col')
- residual: float32 [4, 8, 8], P('row', 'col')
Inputs may be any that keep to these rules, and one draw needn't show every extreme that they name: `micro_counts`: every draw has an element with 12 inner iterations and one with 6.
All inputs are finite; a program needn't handle non-finite values.
Results may differ from a plain program's by a relative error of at most 0.0003.
Values sent between devices are 32-bit elements; how exact they have to be, the bound alone decides.
A program may use at most 64 MiB of HBM per device.

v0:
```python
import jax
import jax.numpy as jnp
from jax import lax
from jax.sharding import PartitionSpec as P

VOX = 24
YZ = 576
PHASES = 3
MACRO_ITERS = 8


def forward(field, axis_id):
    z_index = jnp.arange(YZ) % VOX
    if axis_id == 0:
        return jnp.roll(field, -1, axis=-2)
    if axis_id == 1:
        return jnp.roll(field, -VOX, axis=-1)
    return jnp.where(
        z_index == VOX - 1, jnp.roll(field, VOX - 1, axis=-1), jnp.roll(field, -1, axis=-1)
    )


def behind(field, axis_id):
    z_index = jnp.arange(YZ) % VOX
    if axis_id == 0:
        return jnp.roll(field, 1, axis=-2)
    if axis_id == 1:
        return jnp.roll(field, VOX, axis=-1)
    return jnp.where(z_index == 0, jnp.roll(field, 1 - VOX, axis=-1), jnp.roll(field, 1, axis=-1))


def solve_rve(conduct, count):
    faces = [(conduct + forward(conduct, axis_id)) * 0.5 for axis_id in range(3)]
    back_faces = [behind(faces[axis_id], axis_id) for axis_id in range(3)]
    rhs = jnp.stack([faces[axis_id] - back_faces[axis_id] for axis_id in range(3)])

    def operate(field):
        total = jnp.zeros_like(field)
        for axis_id in range(3):
            total = total + faces[axis_id] * (field - forward(field, axis_id))
            total = total + back_faces[axis_id] * (field - behind(field, axis_id))
        return total

    def sweep(index, carry):
        fluct, remain, direction, norm_now = carry
        image = operate(direction)
        step_size = norm_now / jnp.sum(direction * image, axis=(1, 2))
        fluct = fluct + step_size[:, None, None] * direction
        remain = remain - step_size[:, None, None] * image
        norm_next = jnp.sum(remain * remain, axis=(1, 2))
        direction = remain + (norm_next / norm_now)[:, None, None] * direction
        return (fluct, remain, direction, norm_next)

    start = (jnp.zeros_like(rhs), rhs, rhs, jnp.sum(rhs * rhs, axis=(1, 2)))
    fluct = lax.fori_loop(0, count, sweep, start)[0]
    identity = jnp.eye(3, dtype=conduct.dtype)
    rows_out = []
    for axis_id in range(3):
        flux = faces[axis_id][None] * (
            identity[axis_id][:, None, None] + forward(fluct, axis_id) - fluct
        )
        rows_out.append(jnp.mean(flux, axis=(1, 2)))
    return (fluct, jnp.stack(rows_out))


def solve_batch(conduct, counts):
    return lax.map(lambda pair: solve_rve(pair[0], pair[1]), (conduct, counts))


def neighbour(padded, axis_id, offset):
    lead = padded.ndim - 3
    index = [slice(None)] * lead + [slice(1, -1)] * 3
    length = padded.shape[lead + axis_id]
    index[lead + axis_id] = slice(1 + offset, length - 1 + offset)
    return padded[tuple(index)]


def coarse_apply(k_padded, v_padded):
    centre = neighbour(v_padded, 0, 0)
    total = jnp.zeros_like(centre)
    for axis_id in range(3):
        k_centre = neighbour(k_padded[axis_id], 0, 0)
        for offset in (1, -1):
            cond_face = 0.5 * (k_centre + neighbour(k_padded[axis_id], axis_id, offset))
            total = total + cond_face * (centre - neighbour(v_padded, axis_id, offset))
    return total


def coarse_cg(k_padded, residual, pad_field, norm_of, curv_of):
    increment = jnp.zeros_like(residual)
    direction = residual
    norm_now = norm_of(residual)
    for iteration in range(MACRO_ITERS):
        image = coarse_apply(k_padded, pad_field(direction))
        step_size = norm_now / curv_of(direction, image)
        increment = increment + step_size * direction
        residual = residual - step_size * image
        norm_next = norm_of(residual)
        direction = residual + norm_next / norm_now * direction
        norm_now = norm_next
    return (increment, residual)


def local_norm(field):
    return jnp.sum(field * field)


def local_curv(first, second):
    return jnp.sum(first * second)


def shards(phases, grain, phase_cond, micro_counts, current, load):
    depth = phases.shape[2]
    conduct = jnp.zeros(grain.shape, grain.dtype)
    for phase_id in range(PHASES):
        conduct = conduct + jnp.where(phases == phase_id, phase_cond[phase_id], 0.0)
    conduct = conduct * grain
    flat = conduct.reshape(depth, VOX, YZ)
    counts = micro_counts.reshape(depth)
    fluct, tangent = solve_batch(flat, counts)
    states = fluct.reshape(1, 1, depth, 3, VOX, YZ)
    tangent_out = tangent.reshape(1, 1, depth, 3, 3)
    diag = jnp.stack([tangent[:, axis_id, axis_id] for axis_id in range(3)]).reshape(3, 1, 1, depth)
    packed = jnp.concatenate(
        [diag, current.reshape(1, 1, 1, depth), load.reshape(1, 1, 1, depth)], axis=0
    ).reshape(5, 1, depth)
    whole = lax.all_gather(packed, ("row", "col"), axis=1, tiled=True)
    whole = whole.reshape(5, lax.axis_size("row"), lax.axis_size("col"), depth)
    padded = jnp.pad(whole, ((0, 0), (1, 1), (1, 1), (1, 1)))
    residual = whole[4] - coarse_apply(padded[:3], padded[3])
    increment, residual = coarse_cg(
        padded[:3], residual, lambda field: jnp.pad(field, 1), local_norm, local_curv
    )
    row_at = lax.axis_index("row")
    col_at = lax.axis_index("col")
    zero_at = jnp.zeros((), jnp.int32)
    increment = lax.dynamic_slice(increment, (row_at, col_at, zero_at), (1, 1, depth))
    residual = lax.dynamic_slice(residual, (row_at, col_at, zero_at), (1, 1, depth))
    return (states, tangent_out, increment, residual)


def solution(mesh):
    placed = (
        P("row", "col", None, None, None),
        P("row", "col", None, None, None),
        P(),
        P("row", "col", None),
        P("row", "col", None),
        P("row", "col", None),
    )
    return jax.shard_map(
        shards,
        mesh=mesh,
        in_specs=placed,
        out_specs=(
            P("row", "col", None, None, None, None),
            P("row", "col", None, None, None),
            P("row", "col", None),
            P("row", "col", None),
        ),
        check_vma=False,
    )
```

profile of v0, /device:TPU:0, one launch (start us, length us, event | category | flops | bytes accessed | tf_op | source)
XLA Modules:
  0.0 328.0 jit_solution(11989473639624334039)
XLA Ops:
  0.6 1.4 fusion.241
  2.0 3.3 multiply_bitcast_fusion.3
  5.3 194.7 %while.43 = (s32[]{:T(128)}, f32[8,3,24,576]{3,2,1,0:T(8,128)S(1)}, f32[8,3,3]{2,1,0:T(4,128)S(1)}, f32[8,24,576]{2,1,0:T(8,128)S(1)}, s32[8]{0:T(128)S(1)}, /*i...) while((s32[]{:T(128)}, f32[8,3,24,576]{3,2,1,0:T(8,128)S(1)}, f32[8,3,3]{2,1,0:T(4,128)S(1)}, ...), condition=%wide.region_9.10_spmd, body=%wide.region_0.9_spmd.sunk | while | flops 2898470 | bytes 12391870 | solution.py:67
  6.7 0.6 dynamic_slice.81
  7.3 26.4 %while.44 = (s32[]{:T(128)}, f32[3,24,576]{2,1,0:T(8,128)S(1)}, f32[3,24,576]{2,1,0:T(8,128)S(1)}, f32[3,24,576]{2,1,0:T(8,128)S(1)}, f32[3]{0:T(128)S(1)}, /*in...) while((s32[]{:T(128)}, f32[3,24,576]{2,1,0:T(8,128)S(1)}, ...), condition=%wide.region_5.5_spmd, body=%wide.region_2.4_spmd.sunk | while | flops 1539074 | bytes 5974553 | solution.py:55
  36.5 13.5 %while.44 = (s32[]{:T(128)}, f32[3,24,576]{2,1,0:T(8,128)S(1)}, f32[3,24,576]{2,1,0:T(8,128)S(1)}, f32[3,24,576]{2,1,0:T(8,128)S(1)}, f32[3]{0:T(128)S(1)}, /*in...) while((s32[]{:T(128)}, f32[3,24,576]{2,1,0:T(8,128)S(1)}, ...), condition=%wide.region_5.5_spmd, body=%wide.region_2.4_spmd.sunk | while | flops 1539074 | bytes 5974553 | solution.py:55
  52.2 0.6 dynamic_slice.81
  52.8 24.3 %while.44 = (s32[]{:T(128)}, f32[3,24,576]{2,1,0:T(8,128)S(1)}, f32[3,24,576]{2,1,0:T(8,128)S(1)}, f32[3,24,576]{2,1,0:T(8,128)S(1)}, f32[3]{0:T(128)S(1)}, /*in...) while((s32[]{:T(128)}, f32[3,24,576]{2,1,0:T(8,128)S(1)}, ...), condition=%wide.region_5.5_spmd, body=%wide.region_2.4_spmd.sunk | while | flops 1539074 | bytes 5974553 | solution.py:55
  79.2 0.6 dynamic_slice.81
  79.8 22.1 %while.44 = (s32[]{:T(128)}, f32[3,24,576]{2,1,0:T(8,128)S(1)}, f32[3,24,576]{2,1,0:T(8,128)S(1)}, f32[3,24,576]{2,1,0:T(8,128)S(1)}, f32[3]{0:T(128)S(1)}, /*in...) while((s32[]{:T(128)}, f32[3,24,576]{2,1,0:T(8,128)S(1)}, ...), condition=%wide.region_5.5_spmd, body=%wide.region_2.4_spmd.sunk | while | flops 1539074 | bytes 5974553 | solution.py:55
  104.7 24.3 %while.44 = (s32[]{:T(128)}, f32[3,24,576]{2,1,0:T(8,128)S(1)}, f32[3,24,576]{2,1,0:T(8,128)S(1)}, f32[3,24,576]{2,1,0:T(8,128)S(1)}, f32[3]{0:T(128)S(1)}, /*in...) while((s32[]{:T(128)}, f32[3,24,576]{2,1,0:T(8,128)S(1)}, ...), condition=%wide.region_5.5_spmd, body=%wide.region_2.4_spmd.sunk | while | flops 1539074 | bytes 5974553 | solution.py:55
  131.1 0.6 dynamic_slice.81
  131.7 20.0 %while.44 = (s32[]{:T(128)}, f32[3,24,576]{2,1,0:T(8,128)S(1)}, f32[3,24,576]{2,1,0:T(8,128)S(1)}, f32[3,24,576]{2,1,0:T(8,128)S(1)}, f32[3]{0:T(128)S(1)}, /*in...) while((s32[]{:T(128)}, f32[3,24,576]{2,1,0:T(8,128)S(1)}, ...), condition=%wide.region_5.5_spmd, body=%wide.region_2.4_spmd.sunk | while | flops 1539074 | bytes 5974553 | solution.py:55
  154.4 22.1 %while.44 = (s32[]{:T(128)}, f32[3,24,576]{2,1,0:T(8,128)S(1)}, f32[3,24,576]{2,1,0:T(8,128)S(1)}, f32[3,24,576]{2,1,0:T(8,128)S(1)}, f32[3]{0:T(128)S(1)}, /*in...) while((s32[]{:T(128)}, f32[3,24,576]{2,1,0:T(8,128)S(1)}, ...), condition=%wide.region_5.5_spmd, body=%wide.region_2.4_spmd.sunk | while | flops 1539074 | bytes 5974553 | solution.py:55
  179.3 20.0 %while.44 = (s32[]{:T(128)}, f32[3,24,576]{2,1,0:T(8,128)S(1)}, f32[3,24,576]{2,1,0:T(8,128)S(1)}, f32[3,24,576]{2,1,0:T(8,128)S(1)}, f32[3]{0:T(128)S(1)}, /*in...) while((s32[]{:T(128)}, f32[3,24,576]{2,1,0:T(8,128)S(1)}, ...), condition=%wide.region_5.5_spmd, body=%wide.region_2.4_spmd.sunk | while | flops 1539074 | bytes 5974553 | solution.py:55
  200.3 95.0 %all-gather = f32[5,32,1,8]{3,2,0,1:T(1,128)S(1)} all-gather(f32[5,1,1,8]{3,2,0,1:T(1,128)S(1)} %copy.37), channel_id=2, replica_groups=mesh['row'=4,'col'=8] {'row','col'}, dimensions={1}, use_global_device_ids=true | all-gather | bytes 5280 | tf_op jit(solution)/shard_map/all_gather | solution.py:127
  296.0 0.7 multiply_reduce_fusion.17
  298.0 0.6 multiply_reduce_fusion.16
  300.0 0.7 multiply_reduce_fusion.15
  302.0 0.6 multiply_reduce_fusion.14
  304.0 0.7 multiply_reduce_fusion.13
  306.0 0.6 multiply_reduce_fusion.12
  308.0 0.7 multiply_reduce_fusion.11
  310.0 0.6 multiply_reduce_fusion.10
  312.0 0.7 multiply_reduce_fusion.9
  314.0 0.6 multiply_reduce_fusion.8
  316.0 0.7 multiply_reduce_fusion.7
  318.0 0.6 multiply_reduce_fusion.6
  320.0 0.7 multiply_reduce_fusion.5
  322.0 0.6 multiply_reduce_fusion.4
  324.0 0.7 multiply_reduce_fusion.3
  327.3 0.7 copy.40
  (1556 shorter events, 130.7 us)
Async XLA Ops:
  0.6 4.7 %copy-start.3 = (s32[1,1,8]{2,1,0:T(1,128)S(1)}, s32[1,1,8]{2,1,0:T(1,128)}, u32[]{:S(2)}) copy-start(s32[1,1,8]{2,1,0:T(1,128)} %param.13) | copy-start | bytes 100
  5.3 195.0 %copy-start = (f32[1,1,8]{2,1,0:T(1,128)S(1)}, f32[1,1,8]{2,1,0:T(1,128)}, u32[]{:S(2)}) copy-start(f32[1,1,8]{2,1,0:T(1,128)} %param.15) | copy-start | bytes 100
  5.3 195.0 %copy-start.1 = (f32[1,1,8]{2,1,0:T(1,128)S(1)}, f32[1,1,8]{2,1,0:T(1,128)}, u32[]{:S(2)}) copy-start(f32[1,1,8]{2,1,0:T(1,128)} %param.14) | copy-start | bytes 100
  200.0 124.6 %copy-start.2 = (f32[8,3,24,576]{3,2,1,0:T(8,128)}, f32[8,3,24,576]{3,2,1,0:T(8,128)S(1)}, u32[]{:S(2)}) copy-start(f32[8,3,24,576]{3,2,1,0:T(8,128)S(1)} %get-tuple-element.269) | copy-start | bytes 3981316
where the time goes:
time: 330 us; the launch traced here: 328 us
  blocking collectives  95 us (29%)
  other arithmetic  84.9 us (26%)
  loops' own time  63.8 us (19%)
  local copies, waits for them, and re-layouts  63.4 us (19%)
  between operations  20.9 us (6%)
    all_gather x1, blocking collectives, shards(): whole = lax.all_gather(packed, ('row', 'col'), axis=1, tiled=True)  95 us
    another operation x8, loops' own time, solve_rve(): fluct = lax.fori_loop(0, count, sweep, start)[0]  61.7 us
    reduce_sum x78, other arithmetic, sweep(): step_size = norm_now / jnp.sum(direction * image, axis=(1, 2))  33 us
    reduce_sum x78, other arithmetic, sweep(): norm_next = jnp.sum(remain * remain, axis=(1, 2))  18.5 us
    slice x172, local copies, waits for them, and re-layouts, forward(): return jnp.roll(field, -VOX, axis=-1)  15.7 us
    slice x164, local copies, waits for them, and re-layouts, forward(): jnp.roll(field, VOX - 1, axis=-1)  15.1 us
    slice x172, local copies, waits for them, and re-layouts, forward(): jnp.roll(field, -1, axis=-1)  15 us
    add x78, other arithmetic, sweep(): direction = remain + (norm_next / norm_now)[:, None, None] * direction  10.1 us

commit v1 on v0

--- a/solution.py
+++ b/solution.py
@@ -124,7 +124,8 @@
     packed = jnp.concatenate(
         [diag, current.reshape(1, 1, 1, depth), load.reshape(1, 1, 1, depth)], axis=0
     ).reshape(5, 1, depth)
-    whole = lax.all_gather(packed, ("row", "col"), axis=1, tiled=True)
+    blocks = lax.all_gather(packed, ("row", "col"))
+    whole = jnp.concatenate(blocks, axis=1)
     whole = whole.reshape(5, lax.axis_size("row"), lax.axis_size("col"), depth)
     padded = jnp.pad(whole, ((0, 0), (1, 1), (1, 1), (1, 1)))
     residual = whole[4] - coarse_apply(padded[:3], padded[3])

time: 330 us -> 330 us (level)
  no operation moved by 1% of the time
where the time goes in v1:
time: 330 us; the launch traced here: 329 us
  blocking collectives  95 us (29%)
  other arithmetic  84.9 us (26%)
  local copies, waits for them, and re-layouts  63.8 us (19%)
  loops' own time  63.8 us (19%)
  between operations  20.9 us (6%)
    all_gather x1, blocking collectives, shards(): blocks = lax.all_gather(packed, ('row', 'col'))  95 us
    another operation x8, loops' own time, solve_rve(): fluct = lax.fori_loop(0, count, sweep, start)[0]  61.7 us
    reduce_sum x78, other arithmetic, sweep(): step_size = norm_now / jnp.sum(direction * image, axis=(1, 2))  33 us
    reduce_sum x78, other arithmetic, sweep(): norm_next = jnp.sum(remain * remain, axis=(1, 2))  18.5 us
    slice x172, local copies, waits for them, and re-layouts, forward(): return jnp.roll(field, -VOX, axis=-1)  15.7 us
    slice x164, local copies, waits for them, and re-layouts, forward(): jnp.roll(field, VOX - 1, axis=-1)  15.1 us
    slice x172, local copies, waits for them, and re-layouts, forward(): jnp.roll(field, -1, axis=-1)  15 us
    add x78, other arithmetic, sweep(): direction = remain + (norm_next / norm_now)[:, None, None] * direction  10.1 us

profile of v1, /device:TPU:0, one launch (start us, length us, event | category | flops | bytes accessed | tf_op | source)
XLA Modules:
  0.0 328.5 jit_solution(16228874044277907335)
XLA Ops:
  0.6 1.4 fusion.241
  2.0 3.3 multiply_bitcast_fusion.3
  5.3 194.7 %while.43 = (s32[]{:T(128)}, f32[8,3,24,576]{3,2,1,0:T(8,128)S(1)}, f32[8,3,3]{2,1,0:T(4,128)S(1)}, f32[8,24,576]{2,1,0:T(8,128)S(1)}, s32[8]{0:T(128)S(1)}, /*i...) while((s32[]{:T(128)}, f32[8,3,24,576]{3,2,1,0:T(8,128)S(1)}, f32[8,3,3]{2,1,0:T(4,128)S(1)}, ...), condition=%wide.region_9.10_spmd, body=%wide.region_0.9_spmd.sunk | while | flops 2898470 | bytes 12391870 | solution.py:67
  6.7 0.6 dynamic_slice.81
  7.3 26.4 %while.44 = (s32[]{:T(128)}, f32[3,24,576]{2,1,0:T(8,128)S(1)}, f32[3,24,576]{2,1,0:T(8,128)S(1)}, f32[3,24,576]{2,1,0:T(8,128)S(1)}, f32[3]{0:T(128)S(1)}, /*in...) while((s32[]{:T(128)}, f32[3,24,576]{2,1,0:T(8,128)S(1)}, ...), condition=%wide.region_5.5_spmd, body=%wide.region_2.4_spmd.sunk | while | flops 1539074 | bytes 5974553 | solution.py:55
  36.5 13.5 %while.44 = (s32[]{:T(128)}, f32[3,24,576]{2,1,0:T(8,128)S(1)}, f32[3,24,576]{2,1,0:T(8,128)S(1)}, f32[3,24,576]{2,1,0:T(8,128)S(1)}, f32[3]{0:T(128)S(1)}, /*in...) while((s32[]{:T(128)}, f32[3,24,576]{2,1,0:T(8,128)S(1)}, ...), condition=%wide.region_5.5_spmd, body=%wide.region_2.4_spmd.sunk | while | flops 1539074 | bytes 5974553 | solution.py:55
  52.2 0.6 dynamic_slice.81
  52.8 24.3 %while.44 = (s32[]{:T(128)}, f32[3,24,576]{2,1,0:T(8,128)S(1)}, f32[3,24,576]{2,1,0:T(8,128)S(1)}, f32[3,24,576]{2,1,0:T(8,128)S(1)}, f32[3]{0:T(128)S(1)}, /*in...) while((s32[]{:T(128)}, f32[3,24,576]{2,1,0:T(8,128)S(1)}, ...), condition=%wide.region_5.5_spmd, body=%wide.region_2.4_spmd.sunk | while | flops 1539074 | bytes 5974553 | solution.py:55
  79.2 0.6 dynamic_slice.81
  79.8 22.1 %while.44 = (s32[]{:T(128)}, f32[3,24,576]{2,1,0:T(8,128)S(1)}, f32[3,24,576]{2,1,0:T(8,128)S(1)}, f32[3,24,576]{2,1,0:T(8,128)S(1)}, f32[3]{0:T(128)S(1)}, /*in...) while((s32[]{:T(128)}, f32[3,24,576]{2,1,0:T(8,128)S(1)}, ...), condition=%wide.region_5.5_spmd, body=%wide.region_2.4_spmd.sunk | while | flops 1539074 | bytes 5974553 | solution.py:55
  104.7 24.3 %while.44 = (s32[]{:T(128)}, f32[3,24,576]{2,1,0:T(8,128)S(1)}, f32[3,24,576]{2,1,0:T(8,128)S(1)}, f32[3,24,576]{2,1,0:T(8,128)S(1)}, f32[3]{0:T(128)S(1)}, /*in...) while((s32[]{:T(128)}, f32[3,24,576]{2,1,0:T(8,128)S(1)}, ...), condition=%wide.region_5.5_spmd, body=%wide.region_2.4_spmd.sunk | while | flops 1539074 | bytes 5974553 | solution.py:55
  131.1 0.6 dynamic_slice.81
  131.7 20.0 %while.44 = (s32[]{:T(128)}, f32[3,24,576]{2,1,0:T(8,128)S(1)}, f32[3,24,576]{2,1,0:T(8,128)S(1)}, f32[3,24,576]{2,1,0:T(8,128)S(1)}, f32[3]{0:T(128)S(1)}, /*in...) while((s32[]{:T(128)}, f32[3,24,576]{2,1,0:T(8,128)S(1)}, ...), condition=%wide.region_5.5_spmd, body=%wide.region_2.4_spmd.sunk | while | flops 1539074 | bytes 5974553 | solution.py:55
  154.4 22.1 %while.44 = (s32[]{:T(128)}, f32[3,24,576]{2,1,0:T(8,128)S(1)}, f32[3,24,576]{2,1,0:T(8,128)S(1)}, f32[3,24,576]{2,1,0:T(8,128)S(1)}, f32[3]{0:T(128)S(1)}, /*in...) while((s32[]{:T(128)}, f32[3,24,576]{2,1,0:T(8,128)S(1)}, ...), condition=%wide.region_5.5_spmd, body=%wide.region_2.4_spmd.sunk | while | flops 1539074 | bytes 5974553 | solution.py:55
  179.3 20.0 %while.44 = (s32[]{:T(128)}, f32[3,24,576]{2,1,0:T(8,128)S(1)}, f32[3,24,576]{2,1,0:T(8,128)S(1)}, f32[3,24,576]{2,1,0:T(8,128)S(1)}, f32[3]{0:T(128)S(1)}, /*in...) while((s32[]{:T(128)}, f32[3,24,576]{2,1,0:T(8,128)S(1)}, ...), condition=%wide.region_5.5_spmd, body=%wide.region_2.4_spmd.sunk | while | flops 1539074 | bytes 5974553 | solution.py:55
  200.3 95.0 %all-gather = f32[160,1,1,8]{3,2,1,0:T(1,128)S(1)} all-gather(f32[5,1,1,8]{3,2,1,0:T(1,128)S(1)} %copy.41), channel_id=2, replica_groups=mesh['row'=4,'col'=8] {'row','col'}, dimensions={0}, use_global_device_ids=true | all-gather | bytes 5280 | tf_op jit(solution)/shard_map/all_gather | solution.py:127
  296.5 0.7 multiply_reduce_fusion.17
  298.5 0.6 multiply_reduce_fusion.16
  300.5 0.7 multiply_reduce_fusion.15
  302.5 0.6 multiply_reduce_fusion.14
  304.5 0.7 multiply_reduce_fusion.13
  306.5 0.6 multiply_reduce_fusion.12
  308.5 0.7 multiply_reduce_fusion.11
  310.5 0.6 multiply_reduce_fusion.10
  312.5 0.7 multiply_reduce_fusion.9
  314.5 0.6 multiply_reduce_fusion.8
  316.5 0.7 multiply_reduce_fusion.7
  318.5 0.6 multiply_reduce_fusion.6
  320.5 0.7 multiply_reduce_fusion.5
  322.5 0.6 multiply_reduce_fusion.4
  324.5 0.7 multiply_reduce_fusion.3
  327.8 0.7 copy.44
  (1557 shorter events, 131.2 us)
Async XLA Ops:
  0.6 4.7 %copy-start.3 = (s32[1,1,8]{2,1,0:T(1,128)S(1)}, s32[1,1,8]{2,1,0:T(1,128)}, u32[]{:S(2)}) copy-start(s32[1,1,8]{2,1,0:T(1,128)} %param.13) | copy-start | bytes 100
  5.3 195.0 %copy-start = (f32[1,1,8]{2,1,0:T(1,128)S(1)}, f32[1,1,8]{2,1,0:T(1,128)}, u32[]{:S(2)}) copy-start(f32[1,1,8]{2,1,0:T(1,128)} %param.15) | copy-start | bytes 100
  5.3 195.0 %copy-start.1 = (f32[1,1,8]{2,1,0:T(1,128)S(1)}, f32[1,1,8]{2,1,0:T(1,128)}, u32[]{:S(2)}) copy-start(f32[1,1,8]{2,1,0:T(1,128)} %param.14) | copy-start | bytes 100
  200.0 121.1 %copy-start.2 = (f32[8,3,24,576]{3,2,1,0:T(8,128)}, f32[8,3,24,576]{3,2,1,0:T(8,128)S(1)}, u32[]{:S(2)}) copy-start(f32[8,3,24,576]{3,2,1,0:T(8,128)S(1)} %get-tuple-element.269) | copy-start | bytes 3981316
